TPU v7x, 32 devices: a whole 2x2x4 slice. The times are simulated.
32 devices in a mesh: rows: 8 (over y, x, core), feat: 4 (over z).
Axes of the slice: x: 2, y: 2, z: 4, core: 2. Of those that a mesh axis runs over, the one named last changes fastest.
Arguments:
- bins: int32 [8192, 512], P('rows', 'feat'), may hold values from -2147483648 to 2147483647, as said below
- hessian: float32 [32768], P('rows'), may hold values from 0.05 to 1
- thresholds: float32 [128], replicated, may hold values from 0.02 to 0.98
Outputs:
- cuts: float32 [512, 128], P('feat')
Inputs may be any that keep to these rules, and one draw needn't show every extreme that they name: `bins`: each word holds the bin ids, 0 to 255, of rows 4i to 4i + 3 of one feature, row 4i + k in bits 8k to 8k + 7 of the two's complement word.
All inputs are finite; a program needn't handle non-finite values.
Results may differ from a plain program's by a relative error of at most 0.000065.
Values sent between devices are 32-bit elements; how exact they have to be, the bound alone decides.
A program may use at most 192 MiB of HBM per device.

v0:
```python
import math
import jax
import jax.numpy as jnp
from jax import lax
from jax.sharding import PartitionSpec as P

BINS = 256


def unpack(words):
    parts = [jnp.bitwise_and(jnp.right_shift(words, 8 * k), 255) for k in range(4)]
    stacked = jnp.stack(parts, axis=1)
    return stacked.reshape(words.shape[0] * 4, words.shape[1])


def histogram(columns, weights):
    count, width = columns.shape
    limit = max(8, 1048576 // (width * 16))
    block = math.gcd(count, limit)
    col_blocks = columns.reshape(count // block, block, width)
    wt_blocks = weights.reshape(count // block, block)
    levels = jnp.arange(16, dtype=jnp.int32)

    def add_block(total, item):
        col_part, wt_part = item
        high = jnp.right_shift(col_part, 4)
        low = jnp.bitwise_and(col_part, 15)
        high_hot = jnp.where(high[:, :, None] == levels, wt_part[:, None, None], 0.0)
        low_hot = (low[:, :, None] == levels).astype(jnp.float32)
        joint = jnp.einsum("rkh,rkl->khl", high_hot, low_hot, precision=lax.Precision.HIGHEST)
        return (total + joint, None)

    start = jnp.zeros((width, 16, 16), jnp.float32)
    total, unused = lax.scan(add_block, start, (col_blocks, wt_blocks))
    return total.reshape(width, BINS)


def cut_positions(hist, thresholds):
    cum = jnp.cumsum(hist, axis=1)
    before = cum - hist
    total = cum[:, -1]
    target = thresholds[None, :, None] * total[:, None, None]
    ratio = (target - before[:, None, :]) / (hist[:, None, :] + 1.0)
    return jnp.sum(jnp.clip(ratio, 0.0, 1.0), axis=2)


def local(bins, hessian, thresholds):
    regrouped = lax.all_to_all(bins, "rows", split_axis=1, concat_axis=0, tiled=True)
    weights = lax.all_gather(hessian, "rows", axis=0, tiled=True)
    hist = histogram(unpack(regrouped), weights)
    cuts = cut_positions(hist, thresholds)
    return lax.all_gather(cuts, "rows", axis=0, tiled=True)


def solution(mesh):
    in_specs = (P("rows", "feat"), P("rows"), P())
    out_specs = P("feat", None)
    return jax.shard_map(local, mesh=mesh, in_specs=in_specs, out_specs=out_specs, check_vma=False)
```

profile of v0, /device:TPU:0, one launch (start us, length us, event | category | flops | bytes accessed | tf_op | source)
XLA Modules:
  0.0 84.6 jit_solution(17974510913110473244)
XLA Ops:
  0.0 2.0 %copy.34 = s32[1024,128]{0,1:T(8,128)} copy(s32[1024,128]{1,0:T(8,128)} %param.5) | data formatting | bytes 1048576 | tf_op args[0]
  2.0 5.2 %all-to-all-start = ((s32[1024,8,16]{0,2,1:T(8,128)}), s32[1024,8,16]{0,2,1:T(8,128)S(1)}, u32[]{:S(2)}, u32[]{:S(2)}) async-start(s32[1024,8,16]{0,2,1:T(8,128)} %bitcast), calls=%async_computation | async-start | bytes 1048576 | tf_op jit(solution)/shard_map/all_to_all | solution.py:48
  7.3 13.2 %all_gather.6 = f32[32768]{0:T(1024)S(1)} all-gather(f32[4096]{0:T(1024)S(1)} %copy-done), channel_id=1, replica_groups=mesh['rows'=8,'feat'=4] {'rows'}, dimensions={0}, use_global_device_ids=true | all-gather | bytes 147456 | tf_op jit(solution)/shard_map/all_gather | solution.py:49
  20.5 0.3 and_bitcast_fusion.4
  20.7 0.3 copy.35
  21.1 0.1 and.76
  21.2 0.3 copy.36
  21.5 0.1 and.79
  21.6 0.3 copy.37
  21.9 0.9 %and.82 = s32[8192,1,16]{0,2,1:T(8,128)} reshape(s32[8,1024,16]{1,0,2:T(8,128)S(1)} %copy.37) | data formatting | bytes 1048576 | tf_op jit(solution)/shard_map/and | solution.py:11
  22.8 0.3 copy.38
  23.1 0.9 %and.85 = s32[8192,1,16]{0,2,1:T(8,128)} reshape(s32[8,1024,16]{1,0,2:T(8,128)S(1)} %copy.38) | data formatting | bytes 1048576 | tf_op jit(solution)/shard_map/and | solution.py:11
  24.0 1.3 %pad_add_fusion = s32[8192,4,16]{0,2,1:T(8,128)S(1)} fusion(s32[8192,1,16]{0,2,1:T(8,128)} %and.85, s32[8192,1,16]{0,2,1:T(8,128)} %and.82, s32[8192,1,16]{0,2,1:T(8,128)S(1)} %and.79, s32[8192,1,16]{0,2,1:T(8,128)S(1)} %and.76), kind=kLoop, calls=%fused_computation.14 | loop fusion | flops 1572864 | bytes 4194304 | tf_op jit(solution)/shard_map/stack | solution.py:12
  25.4 10.7 %copy.39 = s32[8192,4,16]{2,1,0:T(4,128)} copy(s32[8192,4,16]{0,2,1:T(8,128)S(1)} %pad_add_fusion) | data formatting | bytes 4194304 | tf_op jit(solution)/shard_map/stack | solution.py:12
  36.1 9.6 %copy.40 = s32[8,4096,16]{1,2,0:T(8,128)S(1)} copy(s32[8,4096,16]{2,1,0:T(8,128)} %bitcast.35) | data formatting | bytes 4194304
  45.7 27.9 %while.12 = (s32[]{:T(128)}, f32[16,16,16]{2,1,0:T(8,128)S(1)}, s32[8,4096,16]{1,2,0:T(8,128)S(1)}, f32[8,4096]{1,0:T(8,128)S(1)}, s32[]{:T(128)}, /*index=5*/s32[]{:T(128)}) while((s32[]{:T(128)}, f32[16,16,16]{2,1,0:T(8,128)S(1)}, s32[8,4096,16]{1,2,0:T(8,128)S(1)}, f32[8,4096]{1,0:T(8,128)S(1)}, s32[]{:T(128)}, ...), condition=%wide.region_1.2_spmd.clone.clone, body=%wide.region_0.1_spmd.clone.clone.sunk | while | flops 204611584 | bytes 1392727 | solution.py:34
  45.8 3.4 %fusion.16 = f32[16,16,16]{2,1,0:T(8,128)S(1)} fusion(s32[4096,16]{0,1:T(8,128)S(1)} %get-tuple-element.126, f32[4096]{0:T(1024)S(1)} %bitcast.36, s32[4096,16]{0,1:T(8,128)S(1)} %get-tuple-element.127, f32[16,16,16]{2,1,0:T(8,128)S(1)} %get-tuple-element.135, pred[]{:T(512)S(6)} %compare.3), kind=kOutput, calls=%fused_computation.9.clone.1 | convolution fusion | flops 204480512 | bytes 573441 | tf_op jit(solution)/shard_map/while/body/eval_jaxpr/rkh,rkl->khl/dot_general | solution.py:30
  49.3 3.4 %fusion.16 = f32[16,16,16]{2,1,0:T(8,128)S(1)} fusion(s32[4096,16]{0,1:T(8,128)S(1)} %get-tuple-element.126, f32[4096]{0:T(1024)S(1)} %bitcast.36, s32[4096,16]{0,1:T(8,128)S(1)} %get-tuple-element.127, f32[16,16,16]{2,1,0:T(8,128)S(1)} %get-tuple-element.135, pred[]{:T(512)S(6)} %compare.3), kind=kOutput, calls=%fused_computation.9.clone.1 | convolution fusion | flops 204480512 | bytes 573441 | tf_op jit(solution)/shard_map/while/body/eval_jaxpr/rkh,rkl->khl/dot_general | solution.py:30
  52.8 3.4 %fusion.16 = f32[16,16,16]{2,1,0:T(8,128)S(1)} fusion(s32[4096,16]{0,1:T(8,128)S(1)} %get-tuple-element.126, f32[4096]{0:T(1024)S(1)} %bitcast.36, s32[4096,16]{0,1:T(8,128)S(1)} %get-tuple-element.127, f32[16,16,16]{2,1,0:T(8,128)S(1)} %get-tuple-element.135, pred[]{:T(512)S(6)} %compare.3), kind=kOutput, calls=%fused_computation.9.clone.1 | convolution fusion | flops 204480512 | bytes 573441 | tf_op jit(solution)/shard_map/while/body/eval_jaxpr/rkh,rkl->khl/dot_general | solution.py:30
  56.2 3.4 %fusion.16 = f32[16,16,16]{2,1,0:T(8,128)S(1)} fusion(s32[4096,16]{0,1:T(8,128)S(1)} %get-tuple-element.126, f32[4096]{0:T(1024)S(1)} %bitcast.36, s32[4096,16]{0,1:T(8,128)S(1)} %get-tuple-element.127, f32[16,16,16]{2,1,0:T(8,128)S(1)} %get-tuple-element.135, pred[]{:T(512)S(6)} %compare.3), kind=kOutput, calls=%fused_computation.9.clone.1 | convolution fusion | flops 204480512 | bytes 573441 | tf_op jit(solution)/shard_map/while/body/eval_jaxpr/rkh,rkl->khl/dot_general | solution.py:30
  59.7 3.4 %fusion.16 = f32[16,16,16]{2,1,0:T(8,128)S(1)} fusion(s32[4096,16]{0,1:T(8,128)S(1)} %get-tuple-element.126, f32[4096]{0:T(1024)S(1)} %bitcast.36, s32[4096,16]{0,1:T(8,128)S(1)} %get-tuple-element.127, f32[16,16,16]{2,1,0:T(8,128)S(1)} %get-tuple-element.135, pred[]{:T(512)S(6)} %compare.3), kind=kOutput, calls=%fused_computation.9.clone.1 | convolution fusion | flops 204480512 | bytes 573441 | tf_op jit(solution)/shard_map/while/body/eval_jaxpr/rkh,rkl->khl/dot_general | solution.py:30
  63.2 3.4 %fusion.16 = f32[16,16,16]{2,1,0:T(8,128)S(1)} fusion(s32[4096,16]{0,1:T(8,128)S(1)} %get-tuple-element.126, f32[4096]{0:T(1024)S(1)} %bitcast.36, s32[4096,16]{0,1:T(8,128)S(1)} %get-tuple-element.127, f32[16,16,16]{2,1,0:T(8,128)S(1)} %get-tuple-element.135, pred[]{:T(512)S(6)} %compare.3), kind=kOutput, calls=%fused_computation.9.clone.1 | convolution fusion | flops 204480512 | bytes 573441 | tf_op jit(solution)/shard_map/while/body/eval_jaxpr/rkh,rkl->khl/dot_general | solution.py:30
  66.7 3.4 %fusion.16 = f32[16,16,16]{2,1,0:T(8,128)S(1)} fusion(s32[4096,16]{0,1:T(8,128)S(1)} %get-tuple-element.126, f32[4096]{0:T(1024)S(1)} %bitcast.36, s32[4096,16]{0,1:T(8,128)S(1)} %get-tuple-element.127, f32[16,16,16]{2,1,0:T(8,128)S(1)} %get-tuple-element.135, pred[]{:T(512)S(6)} %compare.3), kind=kOutput, calls=%fused_computation.9.clone.1 | convolution fusion | flops 204480512 | bytes 573441 | tf_op jit(solution)/shard_map/while/body/eval_jaxpr/rkh,rkl->khl/dot_general | solution.py:30
  70.2 3.4 %fusion.16 = f32[16,16,16]{2,1,0:T(8,128)S(1)} fusion(s32[4096,16]{0,1:T(8,128)S(1)} %get-tuple-element.126, f32[4096]{0:T(1024)S(1)} %bitcast.36, s32[4096,16]{0,1:T(8,128)S(1)} %get-tuple-element.127, f32[16,16,16]{2,1,0:T(8,128)S(1)} %get-tuple-element.135, pred[]{:T(512)S(6)} %compare.3), kind=kOutput, calls=%fused_computation.9.clone.1 | convolution fusion | flops 204480512 | bytes 573441 | tf_op jit(solution)/shard_map/while/body/eval_jaxpr/rkh,rkl->khl/dot_general | solution.py:30
  73.6 0.1 reshape.161
  73.7 0.1 reshape.163
  73.8 0.6 reduce-window.6
  74.4 0.2 slice_reduce_fusion
  74.8 0.2 slice_reduce_fusion.1
  75.0 0.7 clamp_reduce_fusion
  75.7 8.3 %all_gather.7 = f32[128,128]{1,0:T(8,128)S(1)} all-gather(f32[16,128]{1,0:T(8,128)S(1)} %clamp_reduce_fusion), channel_id=1, replica_groups=mesh['rows'=8,'feat'=4] {'rows'}, dimensions={0}, use_global_device_ids=true | all-gather | bytes 73728 | tf_op jit(solution)/shard_map/all_gather | solution.py:52
  84.0 0.6 copy.54
  (29 shorter events, 0.8 us)
Async XLA Ops:
  0.0 7.2 %copy-start = (f32[4096]{0:T(1024)S(1)}, f32[4096]{0:T(1024)}, u32[]{:S(2)}) copy-start(f32[4096]{0:T(1024)} %param.6) | copy-start | bytes 49156
  2.0 18.4 %all-to-all-start = ((s32[1024,8,16]{0,2,1:T(8,128)}), s32[1024,8,16]{0,2,1:T(8,128)S(1)}, u32[]{:S(2)}, u32[]{:S(2)}) async-start(s32[1024,8,16]{0,2,1:T(8,128)} %bitcast), calls=%async_computation | async-start | bytes 1048576 | tf_op jit(solution)/shard_map/all_to_all | solution.py:48
  45.7 29.3 %copy-start.1 = (f32[128]{0:T(128)S(1)}, f32[128]{0:T(128)}, u32[]{:S(2)}) copy-start(f32[128]{0:T(128)} %param.7) | copy-start | bytes 1540
where the time goes:
time: 85 us; the launch traced here: 84.6 us
  matrix products  27.1 us (32%)
  local copies, waits for them, and re-layouts  27 us (32%)
  blocking collectives  21.5 us (25%)
  starting transfers between devices  5.2 us (6%)
  other arithmetic  3.46 us (4%)
    dot_general x8, matrix products, add_block(): jnp.einsum('rkh,rkl->khl', high_hot, low_hot, precision=lax.Precision.HIG...  27.1 us
    all_gather x1, blocking collectives, local(): weights = lax.all_gather(hessian, 'rows', axis=0, tiled=True)  13.2 us
    unnamed x7, local copies, waits for them, and re-layouts  12.3 us
    another operation x1, local copies, waits for them, and re-layouts, unpack(): stacked = jnp.stack(parts, axis=1)  10.7 us
    all_gather x1, blocking collectives, local(): return lax.all_gather(cuts, 'rows', axis=0, tiled=True)  8.29 us
    all_to_all x1, starting transfers between devices, local(): lax.all_to_all(bins, 'rows', split_axis=1, concat_axis=0, tiled=True)  5.2 us
    and x8, local copies, waits for them, and re-layouts, unpack(): jnp.bitwise_and(jnp.right_shift(words, 8 * k), 255)  3.23 us
  transfers between devices with their start and end apart: 1, of which 0 were waited for; matrix products, arithmetic and copies ran while one was open for 0% of the time, Pallas kernels for 0%

commit v1 on v0

--- a/solution.py
+++ b/solution.py
@@ -45,7 +45,10 @@
 
 
 def local(bins, hessian, thresholds):
-    regrouped = lax.all_to_all(bins, "rows", split_axis=1, concat_axis=0, tiled=True)
+    regrouped = jnp.concatenate(
+        lax.all_to_all(jnp.stack(jnp.split(bins, lax.axis_size("rows"), axis=1)), "rows", 0, 0),
+        axis=0,
+    )
     weights = lax.all_gather(hessian, "rows", axis=0, tiled=True)
     hist = histogram(unpack(regrouped), weights)
     cuts = cut_positions(hist, thresholds)

time: 85 us -> 96.5 us (1.14)
  local copies, waits for them, and re-layouts: 27 us -> 38.4 us
    unnamed x7 -> x21, local copies, waits for them, and re-layouts: 12.3 us -> 18.1 us
    split x0 -> x1, local copies, waits for them, and re-layouts: none -> 5.01 us  [local(): jnp.split(bins, lax.axis_size('rows'), axis=1)]
where the time goes in v1:
time: 96.5 us; the launch traced here: 96.1 us
  local copies, waits for them, and re-layouts  38.4 us (40%)
  matrix products  27.1 us (28%)
  blocking collectives  21.5 us (22%)
  starting transfers between devices  5.2 us (5%)
  other arithmetic  3.47 us (4%)
    dot_general x8, matrix products, add_block(): jnp.einsum('rkh,rkl->khl', high_hot, low_hot, precision=lax.Precision.HIG...  27.1 us
    unnamed x21, local copies, waits for them, and re-layouts  18.1 us
    all_gather x1, blocking collectives, local(): weights = lax.all_gather(hessian, 'rows', axis=0, tiled=True)  13.2 us
    another operation x1, local copies, waits for them, and re-layouts, unpack(): stacked = jnp.stack(parts, axis=1)  10.7 us
    all_gather x1, blocking collectives, local(): return lax.all_gather(cuts, 'rows', axis=0, tiled=True)  8.29 us
    all_to_all x1, starting transfers between devices, local(): lax.all_to_all(jnp.stack(jnp.split(bins, lax.axis_size('rows'), axis=1)),...  5.2 us
    split x1, local copies, waits for them, and re-layouts, local(): jnp.split(bins, lax.axis_size('rows'), axis=1)  5.01 us
    and x8, local copies, waits for them, and re-layouts, unpack(): jnp.bitwise_and(jnp.right_shift(words, 8 * k), 255)  3.23 us
  transfers between devices with their start and end apart: 1, of which 0 were waited for; matrix products, arithmetic and copies ran while one was open for 0% of the time, Pallas kernels for 0%

profile of v1, /device:TPU:0, one launch (start us, length us, event | category | flops | bytes accessed | tf_op | source)
XLA Modules:
  0.0 96.1 jit_solution(671744445005483780)
XLA Ops:
  0.0 5.0 %fusion.13 = (s32[1024,16]{1,0:T(8,128)S(1)}, s32[1024,16]{1,0:T(8,128)S(1)}, s32[1024,16]{1,0:T(8,128)S(1)}, s32[1024,16]{1,0:T(8,128)S(1)}, s32[1024,16]{1,0:T...) fusion(s32[1024,128]{1,0:T(8,128)} %param.5), kind=kLoop, calls=%fused_computation.35 | loop fusion | bytes 1048576 | tf_op jit(solution)/shard_map/split | solution.py:49
  5.0 1.2 %copy.65 = s32[1024,16]{0,1:T(8,128)S(1)} copy(s32[1024,16]{1,0:T(8,128)} %get-tuple-element.108) | data formatting | bytes 131072
  6.2 0.6 bitcast_dynamic-update-slice_fusion.7
  6.8 1.2 %copy.66 = s32[1024,16]{0,1:T(8,128)S(1)} copy(s32[1024,16]{1,0:T(8,128)} %get-tuple-element.107) | data formatting | bytes 131072
  9.1 0.6 bitcast_dynamic-update-slice_fusion.6
  9.7 0.6 bitcast_dynamic-update-slice_fusion.5
  10.3 0.6 bitcast_dynamic-update-slice_fusion.4
  11.0 0.6 bitcast_dynamic-update-slice_fusion.3
  11.6 0.6 bitcast_dynamic-update-slice_fusion.2
  12.2 0.6 bitcast_dynamic-update-slice_fusion.1
  12.8 0.6 bitcast_dynamic-update-slice_fusion
  13.5 5.2 %all-to-all-start = ((s32[8,1024,16]{1,2,0:T(8,128)}), s32[8,1024,16]{1,2,0:T(8,128)S(1)}, u32[]{:S(2)}, u32[]{:S(2)}) async-start(s32[8,1024,16]{1,2,0:T(8,128)} %bitcast_dynamic-update-slice_fusion), calls=%async_computation | async-start | bytes 1048576 | tf_op jit(solution)/shard_map/all_to_all | solution.py:49
  18.7 13.2 %all_gather.6 = f32[32768]{0:T(1024)S(1)} all-gather(f32[4096]{0:T(1024)S(1)} %copy-done), channel_id=1, replica_groups=mesh['rows'=8,'feat'=4] {'rows'}, dimensions={0}, use_global_device_ids=true | all-gather | bytes 147456 | tf_op jit(solution)/shard_map/all_gather | solution.py:52
  32.2 0.3 copy.57
  33.3 0.9 and.67
  34.5 0.9 and.69
  35.4 1.3 %pad_add_fusion = s32[8192,4,16]{0,2,1:T(8,128)S(1)} fusion(s32[8192,1,16]{0,2,1:T(8,128)} %and.69, s32[8192,1,16]{0,2,1:T(8,128)} %and.67, s32[8192,1,16]{0,2,1:T(8,128)S(1)} %and.65, s32[8192,1,16]{0,2,1:T(8,128)S(1)} %and.63), kind=kLoop, calls=%fused_computation.14 | loop fusion | flops 1572864 | bytes 4194304 | tf_op jit(solution)/shard_map/stack | solution.py:12
  36.8 10.7 %copy.61 = s32[8192,4,16]{2,1,0:T(4,128)} copy(s32[8192,4,16]{0,2,1:T(8,128)S(1)} %pad_add_fusion) | data formatting | bytes 4194304 | tf_op jit(solution)/shard_map/stack | solution.py:12
  47.5 9.6 %copy.62 = s32[8,4096,16]{1,2,0:T(8,128)S(1)} copy(s32[8,4096,16]{2,1,0:T(8,128)} %bitcast.42) | data formatting | bytes 4194304
  57.1 27.9 %while.12 = (s32[]{:T(128)}, f32[16,16,16]{2,1,0:T(8,128)S(1)}, s32[8,4096,16]{1,2,0:T(8,128)S(1)}, f32[8,4096]{1,0:T(8,128)S(1)}, s32[]{:T(128)}, /*index=5*/s32[]{:T(128)}) while((s32[]{:T(128)}, f32[16,16,16]{2,1,0:T(8,128)S(1)}, s32[8,4096,16]{1,2,0:T(8,128)S(1)}, f32[8,4096]{1,0:T(8,128)S(1)}, s32[]{:T(128)}, ...), condition=%wide.region_1.2_spmd.clone.clone, body=%wide.region_0.1_spmd.clone.clone.sunk | while | flops 204611584 | bytes 1392727 | solution.py:34
  57.2 3.4 %fusion.17 = f32[16,16,16]{2,1,0:T(8,128)S(1)} fusion(s32[4096,16]{0,1:T(8,128)S(1)} %get-tuple-element.138, f32[4096]{0:T(1024)S(1)} %bitcast.43, s32[4096,16]{0,1:T(8,128)S(1)} %get-tuple-element.139, f32[16,16,16]{2,1,0:T(8,128)S(1)} %get-tuple-element.147, pred[]{:T(512)S(6)} %compare.3), kind=kOutput, calls=%fused_computation.9.clone.1 | convolution fusion | flops 204480512 | bytes 573441 | tf_op jit(solution)/shard_map/while/body/eval_jaxpr/rkh,rkl->khl/dot_general | solution.py:30
  60.7 3.4 %fusion.17 = f32[16,16,16]{2,1,0:T(8,128)S(1)} fusion(s32[4096,16]{0,1:T(8,128)S(1)} %get-tuple-element.138, f32[4096]{0:T(1024)S(1)} %bitcast.43, s32[4096,16]{0,1:T(8,128)S(1)} %get-tuple-element.139, f32[16,16,16]{2,1,0:T(8,128)S(1)} %get-tuple-element.147, pred[]{:T(512)S(6)} %compare.3), kind=kOutput, calls=%fused_computation.9.clone.1 | convolution fusion | flops 204480512 | bytes 573441 | tf_op jit(solution)/shard_map/while/body/eval_jaxpr/rkh,rkl->khl/dot_general | solution.py:30
  64.2 3.4 %fusion.17 = f32[16,16,16]{2,1,0:T(8,128)S(1)} fusion(s32[4096,16]{0,1:T(8,128)S(1)} %get-tuple-element.138, f32[4096]{0:T(1024)S(1)} %bitcast.43, s32[4096,16]{0,1:T(8,128)S(1)} %get-tuple-element.139, f32[16,16,16]{2,1,0:T(8,128)S(1)} %get-tuple-element.147, pred[]{:T(512)S(6)} %compare.3), kind=kOutput, calls=%fused_computation.9.clone.1 | convolution fusion | flops 204480512 | bytes 573441 | tf_op jit(solution)/shard_map/while/body/eval_jaxpr/rkh,rkl->khl/dot_general | solution.py:30
  67.7 3.4 %fusion.17 = f32[16,16,16]{2,1,0:T(8,128)S(1)} fusion(s32[4096,16]{0,1:T(8,128)S(1)} %get-tuple-element.138, f32[4096]{0:T(1024)S(1)} %bitcast.43, s32[4096,16]{0,1:T(8,128)S(1)} %get-tuple-element.139, f32[16,16,16]{2,1,0:T(8,128)S(1)} %get-tuple-element.147, pred[]{:T(512)S(6)} %compare.3), kind=kOutput, calls=%fused_computation.9.clone.1 | convolution fusion | flops 204480512 | bytes 573441 | tf_op jit(solution)/shard_map/while/body/eval_jaxpr/rkh,rkl->khl/dot_general | solution.py:30
  71.2 3.4 %fusion.17 = f32[16,16,16]{2,1,0:T(8,128)S(1)} fusion(s32[4096,16]{0,1:T(8,128)S(1)} %get-tuple-element.138, f32[4096]{0:T(1024)S(1)} %bitcast.43, s32[4096,16]{0,1:T(8,128)S(1)} %get-tuple-element.139, f32[16,16,16]{2,1,0:T(8,128)S(1)} %get-tuple-element.147, pred[]{:T(512)S(6)} %compare.3), kind=kOutput, calls=%fused_computation.9.clone.1 | convolution fusion | flops 204480512 | bytes 573441 | tf_op jit(solution)/shard_map/while/body/eval_jaxpr/rkh,rkl->khl/dot_general | solution.py:30
  74.7 3.4 %fusion.17 = f32[16,16,16]{2,1,0:T(8,128)S(1)} fusion(s32[4096,16]{0,1:T(8,128)S(1)} %get-tuple-element.138, f32[4096]{0:T(1024)S(1)} %bitcast.43, s32[4096,16]{0,1:T(8,128)S(1)} %get-tuple-element.139, f32[16,16,16]{2,1,0:T(8,128)S(1)} %get-tuple-element.147, pred[]{:T(512)S(6)} %compare.3), kind=kOutput, calls=%fused_computation.9.clone.1 | convolution fusion | flops 204480512 | bytes 573441 | tf_op jit(solution)/shard_map/while/body/eval_jaxpr/rkh,rkl->khl/dot_general | solution.py:30
  78.1 3.4 %fusion.17 = f32[16,16,16]{2,1,0:T(8,128)S(1)} fusion(s32[4096,16]{0,1:T(8,128)S(1)} %get-tuple-element.138, f32[4096]{0:T(1024)S(1)} %bitcast.43, s32[4096,16]{0,1:T(8,128)S(1)} %get-tuple-element.139, f32[16,16,16]{2,1,0:T(8,128)S(1)} %get-tuple-element.147, pred[]{:T(512)S(6)} %compare.3), kind=kOutput, calls=%fused_computation.9.clone.1 | convolution fusion | flops 204480512 | bytes 573441 | tf_op jit(solution)/shard_map/while/body/eval_jaxpr/rkh,rkl->khl/dot_general | solution.py:30
  81.6 3.4 %fusion.17 = f32[16,16,16]{2,1,0:T(8,128)S(1)} fusion(s32[4096,16]{0,1:T(8,128)S(1)} %get-tuple-element.138, f32[4096]{0:T(1024)S(1)} %bitcast.43, s32[4096,16]{0,1:T(8,128)S(1)} %get-tuple-element.139, f32[16,16,16]{2,1,0:T(8,128)S(1)} %get-tuple-element.147, pred[]{:T(512)S(6)} %compare.3), kind=kOutput, calls=%fused_computation.9.clone.1 | convolution fusion | flops 204480512 | bytes 573441 | tf_op jit(solution)/shard_map/while/body/eval_jaxpr/rkh,rkl->khl/dot_general | solution.py:30
  85.3 0.6 reduce-window.6
  86.5 0.7 clamp_reduce_fusion
  87.2 8.3 %all_gather.7 = f32[128,128]{1,0:T(8,128)S(1)} all-gather(f32[16,128]{1,0:T(8,128)S(1)} %clamp_reduce_fusion), channel_id=1, replica_groups=mesh['rows'=8,'feat'=4] {'rows'}, dimensions={0}, use_global_device_ids=true | all-gather | bytes 73728 | tf_op jit(solution)/shard_map/all_gather | solution.py:55
  95.4 0.6 copy.91
  (45 shorter events, 3.8 us)
Async XLA Ops:
  8.4 10.3 %copy-start = (f32[4096]{0:T(1024)S(1)}, f32[4096]{0:T(1024)}, u32[]{:S(2)}) copy-start(f32[4096]{0:T(1024)} %param.6) | copy-start | bytes 49156
  13.5 18.4 %all-to-all-start = ((s32[8,1024,16]{1,2,0:T(8,128)}), s32[8,1024,16]{1,2,0:T(8,128)S(1)}, u32[]{:S(2)}, u32[]{:S(2)}) async-start(s32[8,1024,16]{1,2,0:T(8,128)} %bitcast_dynamic-update-slice_fusion), calls=%async_computation | async-start | bytes 1048576 | tf_op jit(solution)/shard_map/all_to_all | solution.py:49
  57.1 29.3 %copy-start.1 = (f32[128]{0:T(128)S(1)}, f32[128]{0:T(128)}, u32[]{:S(2)}) copy-start(f32[128]{0:T(128)} %param.7) | copy-start | bytes 1540
